TPU v7x, 16 devices: a 4x2x1 block of a 4x4x8 slice. The times are simulated.
16 devices in a mesh: dp: 4 (over y, z, core), tp: 4 (over x).
Axes of the slice: x: 4, y: 2, z: 1, core: 2. Of those that a mesh axis runs over, the one named last changes fastest.
The devices are a block of a 4x4x8 slice.
Arguments:
- x: bfloat16 [8192, 6144], P('dp'), parts along dimension 0
- w_gate: bfloat16 [6144, 16384], P(None, 'tp')
- w_up: bfloat16 [6144, 16384], P(None, 'tp')
- w_down: bfloat16 [16384, 6144], P('tp')
Outputs:
- output: bfloat16 [8192, 6144], P('dp'), parts along dimension 0
There are 4 independent parts. A program takes and returns all parts, laid end to end along the dimension named above; an argument that names none is the same for every part.
All inputs are finite; a program needn't handle non-finite values.
Results may differ from a plain program's by a relative error of at most 0.016.
Values are sent between devices in bfloat16 or wider.
A program may use at most 768 MiB of HBM per device.

v0:
```python
import jax
import jax.numpy as jnp
from jax import lax
from jax.sharding import PartitionSpec as P


def solution(mesh):
    def step(x, w_gate, w_up, w_down):
        gate = jnp.dot(x, w_gate, preferred_element_type=jnp.float32)
        up = jnp.dot(x, w_up, preferred_element_type=jnp.float32)
        hidden = (jax.nn.silu(gate) * up).astype(jnp.bfloat16)
        term = jnp.dot(hidden, w_down, preferred_element_type=jnp.float32).astype(jnp.bfloat16)
        return lax.psum(term, "tp")

    return jax.shard_map(
        step,
        mesh=mesh,
        in_specs=(P("dp", None), P(None, "tp"), P(None, "tp"), P("tp", None)),
        out_specs=P("dp", None),
        check_vma=False,
    )
```

profile of v0, /device:TPU:112, one launch (start us, length us, event | category | flops | bytes accessed | tf_op | source)
XLA Modules:
  0.0 815.4 jit_solution(5171447726142173224)
XLA Ops:
  6.5 0.0 all-reduce.2.cloned.1.call-start
  6.6 118.0 %fusion = f32[2048,4096]{1,0:T(8,128)} fusion(bf16[2048,6144]{1,0:T(8,128)(2,1)} %param.4, bf16[6144,4096]{1,0:T(8,128)(2,1)} %param.5), kind=kOutput, calls=%fused_computation.2 | convolution fusion | flops 103079215104 | bytes 109051904 | tf_op jit(solution)/shard_map/dot_general | solution.py:9
  124.6 124.5 %multiply_convert_fusion = bf16[2048,4096]{1,0:T(8,128)(2,1)} fusion(f32[2048,4096]{1,0:T(8,128)} %fusion, bf16[2048,6144]{1,0:T(8,128)(2,1)} %param.4, bf16[6144,4096]{1,0:T(8,128)(2,1)} %param.6), kind=kOutput, calls=%fused_computation | convolution fusion | flops 103129546752 | bytes 125829120 | tf_op jit(solution)/shard_map/dot_general | solution.py:10
  249.0 113.6 %convolution_convert_fusion = bf16[2048,6144]{1,0:T(8,128)(2,1)} fusion(bf16[2048,4096]{1,0:T(8,128)(2,1)} %multiply_convert_fusion, bf16[4096,6144]{1,0:T(8,128)(2,1)} %param.7), kind=kOutput, calls=%fused_computation.1 | convolution fusion | flops 103091798016 | bytes 92274688 | tf_op jit(solution)/shard_map/dot_general | solution.py:12
  362.6 0.1 all-reduce.2.cloned.1.call-update
  362.7 424.8 %all-reduce.2.cloned.1.call-done = bf16[2048,6144]{1,0:T(8,128)(2,1)} async-done(((bf16[2048,6144]{1,0:T(8,128)(2,1)}), bf16[2048,6144]{1,0:T(8,128)(2,1)}) %all-reduce.2.cloned.1.call-update) | async-done | bytes 25165840 | tf_op jit(solution)/shard_map/psum | solution.py:13
  787.5 21.0 %copy.6 = bf16[2048,6144]{1,0:T(8,128)(2,1)} copy(bf16[2048,6144]{1,0:T(8,128)(2,1)} %all-reduce.2.cloned.1.call-done) | data formatting | bytes 50331648
Async XLA Ops:
  6.5 781.0 %all-reduce.2.cloned.1.call-start = ((), (), s32[]{:S(2)}) async-start(), calls=%async_computation | async-start | bytes 50331648 | tf_op jit(solution)/shard_map/psum | solution.py:13
Sparse Core Ops, SparseCore 0:
  362.8 424.6 all-reduce.1
where the time goes:
time: 816 us; the launch traced here: 815 us
  waiting for transfers between devices  425 us (52%)
  matrix products  356 us (44%)
  local copies, waits for them, and re-layouts  21 us (3%)
  between operations  13.4 us (2%)
    psum x1, waiting for transfers between devices, step(): return lax.psum(term, 'tp')  425 us
    dot_general x1, matrix products, step(): up = jnp.dot(x, w_up, preferred_element_type=jnp.float32)  124 us
    dot_general x1, matrix products, step(): gate = jnp.dot(x, w_gate, preferred_element_type=jnp.float32)  118 us
    dot_general x1, matrix products, step(): jnp.dot(hidden, w_down, preferred_element_type=jnp.float32)  114 us
    unnamed x1, local copies, waits for them, and re-layouts  21 us
  transfers between devices with their start and end apart: 1, of which 1 were waited for; matrix products, arithmetic and copies ran while one was open for 0% of the time, Pallas kernels for 0%

commit v1 on v0

v1 whole, which is shorter than its diff:
```python
import functools

import jax
import jax.numpy as jnp
from jax import lax
from jax.experimental import pallas as pl
from jax.experimental.pallas import tpu as pltpu
from jax.sharding import PartitionSpec as P

MESH = pl.DeviceIdType.MESH
F32, BF16 = jnp.float32, jnp.bfloat16

BLOCKS = (256, 256, 320, 320, 320, 320, 256)
UNIT = 64
DEPTH = 10
WBUF = 3
TN = 256
TD = 512

SCHEDULE = {
    "pair": [24, 25, 26, 27, 52, 53, 54, 55, 80, 81, 82, 83, 84, 110, 111, 112, 113, 114, 139, 140, 141, 142, 143, 169, 170, 171, 172, 173, 196, 197, 198, 199],
    "own": [31, 33, 34, 35, 59, 60, 61, 62, 87, 90, 91, 92, 93, 117, 118, 119, 120, 121, 145, 148, 149, 150, 151, 176, 177, 178, 179, 180, 200, 201, 202, 203],
    "relay": [37, 39, 41, 43, 64, 65, 67, 69, 93, 95, 96, 98, 100, 122, 123, 125, 127, 129, 151, 152, 154, 156, 158, 182, 184, 186, 189, 192, 204, 205, 206, 207],
    "free": [39, 41, 43, 64, 65, 67, 69, 93, 95, 96, 98, 100, 122, 123, 125, 127, 129, 151, 152, 154, 156, 158, 182, 184, 186, 189, 192, 204, 205, 206, 207, 208],
}
EVENTS = tuple(SCHEDULE)


def pick(index, values):
    total = jnp.int32(0)
    for i, v in enumerate(values):
        if v:
            total = total + jnp.where(index == i, jnp.int32(v), jnp.int32(0))
    return total


def kernel(n, x_ref, wg_ref, wu_ref, wd_ref, y_ref, xv, wv, hv, hold,
           opp_s, dir_s, sum_s, own_s, opp_r, dir_r, sum_r,
           x_sem, w_sem, loc_sem, opp_ss, opp_rs, dir_ss, dir_rs, sum_ss, sum_rs,
           ag_ss, ag_rs, re_ss, re_rs):
    me = lax.axis_index("tp")
    rows, depth_in = x_ref.shape
    hidden, width = wd_ref.shape
    piece = width // n
    nu = rows // UNIT
    gu_steps, dn_steps = hidden // TN, width // TD
    per_piece = dn_steps // n
    steps = gu_steps + dn_steps
    nb = len(BLOCKS)
    total_steps = nb * steps
    last = max(max(v) for v in SCHEDULE.values())
    windows = max(nb, last // steps + 1)
    masks = {e: [sum(1 << (g % steps) for g in v if g // steps == b) for b in range(windows)] for e, v in SCHEDULE.items()}
    starts = {e: [sum(g // steps < b for g in v) for b in range(windows)] for e, v in SCHEDULE.items()}
    row0 = [sum(BLOCKS[:b]) for b in range(nb)]

    def at(offset):
        return lax.rem(me + offset, n)

    def remote(src, dst, ssem, rsem, target):
        return pltpu.make_async_remote_copy(src_ref=src, dst_ref=dst, send_sem=ssem, recv_sem=rsem,
                                            device_id={"tp": target}, device_id_type=MESH)

    def cols(owner):
        return pl.ds(pl.multiple_of(owner * piece, piece), piece)

    def unit_rows(s):
        return pl.ds(pl.multiple_of(s * UNIT, UNIT), UNIT)

    def gu_copies(t, slot):
        c = pl.ds(pl.multiple_of(t * TN, TN), TN)
        return (pltpu.make_async_copy(wg_ref.at[:, c], wv.at[slot, :, 0:TN], w_sem.at[slot, 0]),
                pltpu.make_async_copy(wu_ref.at[:, c], wv.at[slot, :, TN:2 * TN], w_sem.at[slot, 1]))

    def dn_copy(t, slot):
        p, j = t // per_piece, lax.rem(t, per_piece)
        c = pl.ds(pl.multiple_of(at(pick(p, (2, 1, 3, 0))) * piece + j * TD, TD), TD)
        return pltpu.make_async_copy(wd_ref.at[:, c], wv.at[slot, 0:hidden, :], w_sem.at[slot, 0])

    def start_gu(t, slot):
        for c in gu_copies(t, slot):
            c.start()

    def x_copy(b, r):
        return pltpu.make_async_copy(x_ref.at[pl.ds(pl.multiple_of(pick(b, row0), UNIT), r), :], xv.at[pl.ds(0, r), :], x_sem)

    def opp_copy(s, slot, par, c):
        return remote(opp_s.at[slot, :, c], opp_r.at[slot, :, c], opp_ss.at[slot], opp_rs.at[slot], at(1 + 2 * par))

    def dir_copy(s, slot, par):
        return remote(dir_s.at[slot], dir_r.at[slot], dir_ss.at[slot], dir_rs.at[slot], at(3 - 2 * par))

    def sum_copy(s, slot, par):
        return remote(sum_s.at[slot], sum_r.at[slot], sum_ss.at[slot], sum_rs.at[slot], at(1 + 2 * par))

    def own_copy(s, slot, side):
        return remote(own_s.at[slot], y_ref.at[unit_rows(s), cols(me)], ag_ss.at[slot, side], ag_rs.at[s, side], at(1 + 2 * side))

    def relay_copy(s, par):
        view = y_ref.at[unit_rows(s), cols(at(3 - 2 * par))]
        return remote(view, view, re_ss.at[s], re_rs.at[s], at(1 + 2 * par))

    def loc_copy(s, slot):
        return pltpu.make_async_copy(own_s.at[slot], y_ref.at[unit_rows(s), cols(me)], loc_sem.at[slot])

    whole = pl.ds(0, piece)

    def pair(s):
        slot, par = lax.rem(s, DEPTH), lax.rem(s, 2)
        opp_copy(s, slot, par, whole).wait_recv()
        sum_s[slot] = (hold[slot, 1 + par] + opp_r[slot].astype(F32)).astype(BF16)
        sum_copy(s, slot, par).start()

    def own(s):
        slot, par = lax.rem(s, DEPTH), lax.rem(s, 2)
        dir_copy(s, slot, par).wait_recv()
        sum_copy(s, slot, par).wait_recv()
        own_s[slot] = (hold[slot, 3] + sum_r[slot].astype(F32) + dir_r[slot].astype(F32)).astype(BF16)
        own_copy(s, slot, 0).start()
        own_copy(s, slot, 1).start()
        loc_copy(s, slot).start()

    def relay(s):
        slot, par = lax.rem(s, DEPTH), lax.rem(s, 2)
        own_copy(s, slot, 0).wait_recv()
        own_copy(s, slot, 1).wait_recv()
        relay_copy(s, par).start()

    def free(s):
        slot, par = lax.rem(s, DEPTH), lax.rem(s, 2)
        opp_copy(s, slot, par, whole).wait_send()
        dir_copy(s, slot, par).wait_send()
        sum_copy(s, slot, par).wait_send()
        own_copy(s, slot, 0).wait_send()
        own_copy(s, slot, 1).wait_send()
        loc_copy(s, slot).wait()

    actions = {"pair": pair, "own": own, "relay": relay, "free": free}

    def events(t, mask, done):
        out = []
        for e in EVENTS:
            hit = lax.shift_right_logical(mask[e], t) & 1

            @pl.when(hit == 1)
            def _(e=e, c=done[len(out)]):
                actions[e](c)

            out.append(done[len(out)] + hit)
        return tuple(out)

    x_copy(jnp.int32(0), BLOCKS[0]).start()
    for t in range(WBUF - 1):
        start_gu(jnp.int32(t), jnp.int32(t))
    barrier = pltpu.get_barrier_semaphore()
    for offset in (1, n - 1):
        pl.semaphore_signal(barrier, inc=1, device_id={"tp": at(offset)}, device_id_type=MESH)
    pl.semaphore_wait(barrier, 2)

    def block(b, r):
        units = r // UNIT
        first = pick(b, [v // UNIT for v in row0])
        base = b * steps
        mask = {e: pick(b, masks[e]) for e in EVENTS}
        done = tuple(pick(b, starts[e]) for e in EVENTS)
        x_copy(b, r).wait()

        def gu_step(t, done):
            slot = lax.rem(base + t, WBUF)
            for c in gu_copies(t, slot):
                c.wait()
            ahead = t + WBUF - 1
            later = lax.rem(base + ahead, WBUF)

            @pl.when(ahead < gu_steps)
            def _():
                start_gu(ahead, later)

            @pl.when(ahead >= gu_steps)
            def _():
                dn_copy(ahead - gu_steps, later).start()

            xb = xv[0:r, :]
            gate = jnp.dot(xb, wv[slot, :, 0:TN], preferred_element_type=F32)
            up = jnp.dot(xb, wv[slot, :, TN:2 * TN], preferred_element_type=F32)
            hv[0:r, pl.ds(pl.multiple_of(t * TN, TN), TN)] = (jax.nn.silu(gate) * up).astype(BF16)
            return events(t, mask, done)

        done = lax.fori_loop(0, gu_steps, gu_step, done)
        for r2 in sorted(set(BLOCKS)):
            @pl.when(pick(b + 1, [v == r2 for v in BLOCKS]) == 1)
            def _(r2=r2):
                x_copy(b + 1, r2).start()

        def dn_step(t, done):
            g = base + gu_steps + t
            slot = lax.rem(g, WBUF)
            dn_copy(t, slot).wait()
            ahead = t + WBUF - 1
            later = lax.rem(g + WBUF - 1, WBUF)

            @pl.when(ahead < dn_steps)
            def _():
                dn_copy(ahead, later).start()

            @pl.when((ahead >= dn_steps) & (b + 1 < nb))
            def _():
                start_gu(ahead - dn_steps, later)

            p, j = t // per_piece, lax.rem(t, per_piece)
            c = pl.ds(pl.multiple_of(j * TD, TD), TD)
            term = jnp.dot(hv[0:r, :], wv[slot, 0:hidden, :], preferred_element_type=F32)
            for k in range(units):
                hold[lax.rem(first + k, DEPTH), p, :, c] = term[k * UNIT:(k + 1) * UNIT, :]

            @pl.when(p == 0)
            def _():
                def send(k, _):
                    s = first + k
                    slot, par = lax.rem(s, DEPTH), lax.rem(s, 2)
                    opp_s[slot, :, c] = hold[slot, 0, :, c].astype(BF16)
                    opp_copy(s, slot, par, c).start()
                    return 0
                lax.fori_loop(0, units, send, 0)

            @pl.when((j == per_piece - 1) & ((p == 1) | (p == 2)))
            def _():
                def send(k, _):
                    s = first + k
                    slot, par = lax.rem(s, DEPTH), lax.rem(s, 2)

                    @pl.when(p == 2 - par)
                    def _():
                        dir_s[slot] = hold[slot, 2 - par].astype(BF16)
                        dir_copy(s, slot, par).start()
                    return 0
                lax.fori_loop(0, units, send, 0)

            return events(gu_steps + t, mask, done)

        lax.fori_loop(0, dn_steps, dn_step, done)

    def outer(b, _):
        for r in sorted(set(BLOCKS)):
            @pl.when(pick(b, [v == r for v in BLOCKS]) == 1)
            def _(r=r):
                block(b, r)
        return 0

    lax.fori_loop(0, nb, outer, 0)

    def tail(g, done):
        b = g // steps
        return events(lax.rem(g, steps), {e: pick(b, masks[e]) for e in EVENTS}, done)

    lax.fori_loop(total_steps, last + 1, tail, tuple(jnp.int32(sum(g < total_steps for g in v)) for v in SCHEDULE.values()))

    def drain(s, _):
        par = lax.rem(s, 2)
        relay_copy(s, par).wait()
        return 0

    lax.fori_loop(0, nu, drain, 0)


def solution(mesh):
    n = mesh.shape["tp"]

    def step(x, w_gate, w_up, w_down):
        rows, din = x.shape
        hidden, width = w_down.shape
        piece = width // n
        rmax = max(BLOCKS)
        ring = pltpu.VMEM((DEPTH, UNIT, piece), BF16)
        dma = pltpu.SemaphoreType.DMA
        return pl.pallas_call(
            functools.partial(kernel, n),
            out_shape=jax.ShapeDtypeStruct((rows, width), BF16),
            in_specs=[pl.BlockSpec(memory_space=pl.ANY)] * 4,
            out_specs=pl.BlockSpec(memory_space=pl.ANY),
            scratch_shapes=[
                pltpu.VMEM((rmax, din), BF16),
                pltpu.VMEM((WBUF, din, 2 * TN), BF16),
                pltpu.VMEM((rmax, hidden), BF16),
                pltpu.VMEM((DEPTH, n, UNIT, piece), F32),
                ring, ring, ring, ring, ring, ring, ring,
                dma, dma((WBUF, 2)), dma((DEPTH,)),
                dma((DEPTH,)), dma((DEPTH,)), dma((DEPTH,)), dma((DEPTH,)), dma((DEPTH,)), dma((DEPTH,)),
                dma((DEPTH, 2)), dma((rows // UNIT, 2)), dma((rows // UNIT,)), dma((rows // UNIT,)),
            ],
            compiler_params=pltpu.CompilerParams(
                collective_id=0, has_side_effects=True, vmem_limit_bytes=63 * 2**20),
            cost_estimate=pl.CostEstimate(flops=6 * rows * din * hidden, bytes_accessed=7 * 6 * din * hidden, transcendentals=0),
        )(x, w_gate, w_up, w_down)

    return jax.shard_map(
        step,
        mesh=mesh,
        in_specs=(P("dp", None), P(None, "tp"), P(None, "tp"), P("tp", None)),
        out_specs=P("dp", None),
        check_vma=False,
    )
```

time: 816 us -> 475 us (0.58)
  Pallas kernels: 0 us -> 454 us
  waiting for transfers between devices: 425 us -> 0 us
  matrix products: 356 us -> 0 us
  between operations: 13.4 us -> 0.01 us
    pallas_call x0 -> x1, Pallas kernels: none -> 454 us  [step(): pl.pallas_call(functools.partial(kernel, n), out_shape=jax.ShapeDtypeStru...]
    psum x1 -> x0, waiting for transfers between devices: 425 us -> none  [step(): return lax.psum(term, 'tp')]
    dot_general x3 -> x0, matrix products: 356 us -> none  [the longest x1 124 us: step(): up = jnp.dot(x, w_up, preferred_element_type=jnp.float32)]
  transfers between devices with their start and end apart: 1 -> 0, of which waited for: 1 -> 0; matrix products, arithmetic and copies ran while one was open for 0% -> 0% of each run, Pallas kernels for 0% -> 0%
where the time goes in v1:
time: 475 us
  Pallas kernels  454 us (96%)
  local copies, waits for them, and re-layouts  21 us (4%)
    pallas_call x1, Pallas kernels, step(): pl.pallas_call(functools.partial(kernel, n), out_shape=jax.ShapeDtypeStru...  454 us
    unnamed x1, local copies, waits for them, and re-layouts  21 us

profile of v1, /device:TPU:112, one launch (start us, length us, event | category | flops | bytes accessed | tf_op | source)
XLA Modules:
  0.0 475.0 jit_solution(817603703849178569)
XLA Ops:
  0.0 454.0 %shard_map.46 = bf16[2048,6144]{1,0:T(8,128)(2,1)} custom-call(bf16[2048,6144]{1,0:T(8,128)(2,1)} %x_ref.1, bf16[6144,4096]{1,0:T(8,128)(2,1)} %wg_ref.1, bf16[6144,4096]{1,0:T(8,128)(2,1)} %wu_ref.1, bf16[4096,6144]{1,0:T(8,128)(2,1)} %wd_ref.1), custom_call_target="tpu_custom_call" | custom-call | flops 309237645312 | bytes 1056964608 | tf_op jit(solution)/shard_map/pallas_call | solution.py:276
  454.0 21.0 %copy.6 = bf16[2048,6144]{1,0:T(8,128)(2,1)} copy(bf16[2048,6144]{1,0:T(8,128)(2,1)} %shard_map.46) | data formatting | bytes 50331648

commit v2 on v1

v2 whole, which is shorter than its diff:
```python
import functools

import jax
import jax.numpy as jnp
from jax import lax
from jax.experimental import pallas as pl
from jax.experimental.pallas import tpu as pltpu
from jax.sharding import PartitionSpec as P

MESH = pl.DeviceIdType.MESH
F32, BF16 = jnp.float32, jnp.bfloat16

BLOCKS = (256, 256, 320, 320, 320, 320, 256)
UNIT = 64
DEPTH = 10
WBUF = 3
TN = 256
TD = 768
TAIL = 8
CHUNK = 128

SCHEDULE = {
    "pair": [21, 22, 23, 24, 47, 48, 49, 50, 69, 70, 71, 72, 73, 94, 96, 97, 98, 99, 119, 120, 121, 122, 123, 145, 146, 147, 148, 149, 169, 170, 171, 172],
    "own": [28, 29, 31, 32, 53, 54, 55, 56, 76, 77, 78, 79, 80, 101, 104, 105, 106, 107, 128, 129, 130, 131, 132, 156, 160, 161, 162, 163, 176, 177, 178, 179],
    "relay": [33, 35, 37, 40, 57, 59, 60, 62, 81, 83, 85, 86, 88, 107, 109, 111, 113, 114, 134, 135, 137, 139, 140, 163, 168, 173, 174, 175, 180, 181, 182, 183],
    "free": [35, 37, 40, 57, 59, 60, 62, 81, 83, 85, 86, 88, 107, 109, 111, 113, 114, 134, 135, 137, 139, 140, 163, 168, 173, 174, 175, 180, 181, 182, 183, 184],
}
EVENTS = tuple(SCHEDULE)


def pick(index, values):
    total = jnp.int32(0)
    for i, v in enumerate(values):
        if v:
            total = total + jnp.where(index == i, jnp.int32(v), jnp.int32(0))
    return total


def kernel(n, x_ref, wg_ref, wu_ref, wd_ref, y_ref, rel_r_ref, rel_l_ref, xv, wv, hv, hold,
           opp_s, dir_s, sum_s, own_s, opp_r, dir_r, sum_r,
           x_sem, w_sem, out_sem, opp_rs, own_rs, ag_rs, re_ss, re_rs):
    me = lax.axis_index("tp")
    rows, depth_in = x_ref.shape
    hidden, width = wd_ref.shape
    piece = width // n
    nu = rows // UNIT
    kept = nu - TAIL
    gu_steps, dn_steps = hidden // TN, width // TD
    per_piece = dn_steps // n
    steps = gu_steps + dn_steps
    nb = len(BLOCKS)
    total_steps = nb * steps
    last = max(max(v) for v in SCHEDULE.values())
    windows = max(nb, last // steps + 1)
    masks = {e: [sum(1 << (g % steps) for g in v if g // steps == b) for b in range(windows)] for e, v in SCHEDULE.items()}
    starts = {e: [sum(g // steps < b for g in v) for b in range(windows)] for e, v in SCHEDULE.items()}
    mid = {e: [sum(g // steps < b or (g // steps == b and g % steps < gu_steps) for g in v) for b in range(windows)] for e, v in SCHEDULE.items()}
    row0 = [sum(BLOCKS[:b]) for b in range(nb)]

    def at(offset):
        return lax.rem(me + offset, n)

    def remote(src, dst, ssem, rsem, target):
        return pltpu.make_async_remote_copy(src_ref=src, dst_ref=dst, send_sem=ssem, recv_sem=rsem,
                                            device_id={"tp": target}, device_id_type=MESH)

    def cols(owner):
        return pl.ds(pl.multiple_of(owner * piece, piece), piece)

    def unit_rows(s):
        return pl.ds(pl.multiple_of(s * UNIT, UNIT), UNIT)

    def gu_copies(t, slot):
        c = pl.ds(pl.multiple_of(t * TN, TN), TN)
        return (pltpu.make_async_copy(wg_ref.at[:, c], wv.at[slot, :, 0:TN], w_sem.at[slot]),
                pltpu.make_async_copy(wu_ref.at[:, c], wv.at[slot, :, TN:2 * TN], w_sem.at[slot]))

    side, half = TD - 2 * TN, hidden // 2

    def dn_copies(t, slot):
        p, j = t // per_piece, lax.rem(t, per_piece)
        c = at(pick(p, (2, 1, 3, 0))) * piece + j * TD
        main = pl.ds(pl.multiple_of(c, TN), 2 * TN)
        rest = pl.ds(pl.multiple_of(c + 2 * TN, TN), side)
        return (pltpu.make_async_copy(wd_ref.at[:, main], wv.at[slot, 0:hidden, :], w_sem.at[slot]),
                pltpu.make_async_copy(wd_ref.at[0:half, rest], wv.at[slot, hidden:hidden + half, 0:side], w_sem.at[slot]),
                pltpu.make_async_copy(wd_ref.at[half:hidden, rest], wv.at[slot, hidden:hidden + half, side:2 * side], w_sem.at[slot]))

    def start_dn(t, slot):
        for c in dn_copies(t, slot):
            c.start()

    def tile_wait(slot):
        pltpu.make_async_copy(wv.at[slot], wv.at[slot], w_sem.at[slot]).wait()

    def start_gu(t, slot):
        for c in gu_copies(t, slot):
            c.start()

    def x_copy(b, r):
        return pltpu.make_async_copy(x_ref.at[pl.ds(pl.multiple_of(pick(b, row0), UNIT), r), :], xv.at[pl.ds(0, r), :], x_sem)

    def opp_copy(s, slot, par, c):
        return remote(opp_s.at[slot, :, c], opp_r.at[slot, :, c], out_sem.at[slot], opp_rs.at[slot], at(1 + 2 * par))

    def dir_copy(s, slot, par, c):
        return remote(dir_s.at[slot, :, c], dir_r.at[slot, :, c], out_sem.at[slot], own_rs.at[slot], at(3 - 2 * par))

    def sum_copy(s, slot, par):
        return remote(sum_s.at[slot], sum_r.at[slot], out_sem.at[slot], own_rs.at[slot], at(1 + 2 * par))

    def own_copy(s, slot, side):
        return remote(own_s.at[slot], y_ref.at[unit_rows(s), cols(me)], out_sem.at[slot], ag_rs.at[slot], at(1 + 2 * side))

    def keep_copy(s, slot, side):
        rel = (rel_r_ref, rel_l_ref)[side].at[(s - kept) // 2]
        return remote(own_s.at[slot], rel, out_sem.at[slot], ag_rs.at[slot], at(1 + 2 * side))

    def relay_copy(s, par):
        view = y_ref.at[unit_rows(s), cols(at(3 - 2 * par))]
        k = lax.rem(s, DEPTH + TAIL)
        return remote(view, view, re_ss.at[k], re_rs.at[k], at(1 + 2 * par))

    def loc_copy(s, slot):
        return pltpu.make_async_copy(own_s.at[slot], y_ref.at[unit_rows(s), cols(me)], out_sem.at[slot])

    whole = pl.ds(0, piece)

    def arrived(sem, pieces):
        size = hold.at[0, 0:pieces // 2]
        pltpu.make_async_copy(size, size, sem).wait()

    def pair(s):
        slot, par = lax.rem(s, DEPTH), lax.rem(s, 2)
        opp_copy(s, slot, par, whole).wait_recv()
        sum_s[slot] = (hold[slot, 1 + par] + opp_r[slot].astype(F32)).astype(BF16)
        sum_copy(s, slot, par).start()

    def own(s):
        slot, par = lax.rem(s, DEPTH), lax.rem(s, 2)
        arrived(own_rs.at[slot], 2)
        own_s[slot] = (hold[slot, 3] + sum_r[slot].astype(F32) + dir_r[slot].astype(F32)).astype(BF16)
        for side in (0, 1):
            keep = (s >= kept) & (par == side)

            @pl.when(keep)
            def _(side=side):
                keep_copy(s, slot, side).start()

            @pl.when(jnp.logical_not(keep))
            def _(side=side):
                own_copy(s, slot, side).start()
        loc_copy(s, slot).start()

    def relay(s):
        slot, par = lax.rem(s, DEPTH), lax.rem(s, 2)
        arrived(ag_rs.at[slot], 2)

        @pl.when(s < kept)
        def _():
            relay_copy(s, par).start()

    def free(s):
        slot, par = lax.rem(s, DEPTH), lax.rem(s, 2)
        arrived(out_sem.at[slot], 6)

        @pl.when((s >= TAIL) & (s < kept + TAIL))
        def _():
            relay_copy(s - TAIL, par).wait()

    actions = {"pair": pair, "own": own, "relay": relay, "free": free}

    def events(t, mask, done):
        out = []
        for e in EVENTS:
            hit = lax.shift_right_logical(mask[e], t) & 1

            @pl.when(hit == 1)
            def _(e=e, c=done[len(out)]):
                actions[e](c)

            out.append(done[len(out)] + hit)
        return tuple(out)

    def state(b):
        return {e: pick(b, masks[e]) for e in EVENTS}, b * steps

    def gu_phase(b, r, exchange=True):
        mask, base = state(b)
        x_copy(b, r).wait()
        if not exchange:
            start_gu(jnp.int32(1), jnp.int32(1))

        def gu_step(t, done):
            slot = lax.rem(base + t, WBUF)
            tile_wait(slot)
            ahead = t + WBUF - 1
            later = lax.rem(base + ahead, WBUF)

            @pl.when(ahead < gu_steps)
            def _():
                start_gu(ahead, later)

            @pl.when(ahead >= gu_steps)
            def _():
                start_dn(ahead - gu_steps, later)

            xb = xv[0:r, :]
            gate = jnp.dot(xb, wv[slot, :, 0:TN], preferred_element_type=F32)
            up = jnp.dot(xb, wv[slot, :, TN:2 * TN], preferred_element_type=F32)
            hv[0:r, pl.ds(pl.multiple_of(t * TN, TN), TN)] = (jax.nn.silu(gate) * up).astype(BF16)
            return events(t, mask, done) if exchange else done

        lax.fori_loop(0, gu_steps, gu_step, tuple(pick(b, starts[e]) for e in EVENTS))

    def dn_phase(b, r):
        units = r // UNIT
        first = pick(b, [v // UNIT for v in row0])
        mask, base = state(b)
        for r2 in sorted(set(BLOCKS)):
            @pl.when(pick(b + 1, [v == r2 for v in BLOCKS]) == 1)
            def _(r2=r2):
                x_copy(b + 1, r2).start()

        def dn_step(t, done):
            g = base + gu_steps + t
            slot = lax.rem(g, WBUF)
            tile_wait(slot)
            ahead = t + WBUF - 1
            later = lax.rem(g + WBUF - 1, WBUF)

            @pl.when(ahead < dn_steps)
            def _():
                start_dn(ahead, later)

            @pl.when((ahead >= dn_steps) & (b + 1 < nb))
            def _():
                start_gu(ahead - dn_steps, later)

            p, j = t // per_piece, lax.rem(t, per_piece)
            c = pl.ds(pl.multiple_of(j * TD, TD), TD)
            term = jnp.dot(hv[0:r, :], wv[slot, 0:hidden, :], preferred_element_type=F32)
            rest = (jnp.dot(hv[0:r, 0:half], wv[slot, hidden:hidden + half, 0:side], preferred_element_type=F32)
                    + jnp.dot(hv[0:r, half:hidden], wv[slot, hidden:hidden + half, side:2 * side], preferred_element_type=F32))
            c0 = pl.ds(pl.multiple_of(j * TD, TN), 2 * TN)
            c1 = pl.ds(pl.multiple_of(j * TD + 2 * TN, TN), side)
            for k in range(units):
                hold[lax.rem(first + k, DEPTH), p, :, c0] = term[k * UNIT:(k + 1) * UNIT, :]
                hold[lax.rem(first + k, DEPTH), p, :, c1] = rest[k * UNIT:(k + 1) * UNIT, :]

            @pl.when(p == 0)
            def _():
                def send(k, _):
                    s = first + k
                    slot, par = lax.rem(s, DEPTH), lax.rem(s, 2)
                    opp_s[slot, :, c] = hold[slot, 0, :, c].astype(BF16)
                    opp_copy(s, slot, par, c).start()
                    return 0
                lax.fori_loop(0, units, send, 0)

            @pl.when((p == 1) | (p == 2))
            def _():
                def send(k, _):
                    s = first + k
                    slot, par = lax.rem(s, DEPTH), lax.rem(s, 2)

                    @pl.when(p == 2 - par)
                    def _():
                        dir_s[slot, :, c] = hold[slot, p, :, c].astype(BF16)
                        dir_copy(s, slot, par, c).start()
                    return 0
                lax.fori_loop(0, units, send, 0)

            return events(gu_steps + t, mask, done)

        lax.fori_loop(0, dn_steps, dn_step, tuple(pick(b, mid[e]) for e in EVENTS))

    def switch(b, phase):
        for r in sorted(set(BLOCKS)):
            @pl.when(pick(b, [v == r for v in BLOCKS]) == 1)
            def _(r=r):
                phase(b, r)

    barrier = pltpu.get_barrier_semaphore()
    for offset in (1, n - 1):
        pl.semaphore_signal(barrier, inc=1, device_id={"tp": at(offset)}, device_id_type=MESH)
    x_copy(jnp.int32(0), BLOCKS[0]).start()
    start_gu(jnp.int32(0), jnp.int32(0))
    gu_phase(jnp.int32(0), BLOCKS[0], exchange=False)
    pl.semaphore_wait(barrier, 2)

    def outer(b, _):
        switch(b, dn_phase)
        switch(b + 1, gu_phase)
        return 0

    lax.fori_loop(0, nb, outer, 0)

    def tail(g, done):
        b = g // steps
        return events(lax.rem(g, steps), {e: pick(b, masks[e]) for e in EVENTS}, done)

    lax.fori_loop(total_steps, last + 1, tail, tuple(jnp.int32(sum(g < total_steps for g in v)) for v in SCHEDULE.values()))


def copy_kernel(n, y_ref, rel_r_ref, rel_l_ref, out_ref, rows_v, units_v, r_sem, w_sem, ur_sem, uw_sem):
    me = lax.axis_index("tp")
    rows, width = y_ref.shape
    piece = width // n
    full = rows - TAIL * UNIT
    jobs = []
    for i in range(full // CHUNK):
        r = pl.ds(i * CHUNK, CHUNK)
        jobs.append((y_ref.at[r, :], rows_v.at[i], out_ref.at[r, :], r_sem.at[i], w_sem.at[i]))
    for i in range(TAIL):
        r = pl.ds(full + i * UNIT, UNIT)
        for k, offset in enumerate((0, 1, n - 1)):
            c = pl.ds(pl.multiple_of(lax.rem(me + offset, n) * piece, piece), piece)
            src = y_ref.at[r, c]
            if offset == n - 1 and i % 2 == 0:
                src = rel_r_ref.at[i // 2]
            if offset == 1 and i % 2 == 1:
                src = rel_l_ref.at[i // 2]
            jobs.append((src, units_v.at[i, k], out_ref.at[r, c], ur_sem.at[i, k], uw_sem.at[i, k]))
    for src, buf, dst, rs, ws in jobs:
        pltpu.make_async_copy(src, buf, rs).start()
    for src, buf, dst, rs, ws in jobs:
        pltpu.make_async_copy(src, buf, rs).wait()
        pltpu.make_async_copy(buf, dst, ws).start()
    for src, buf, dst, rs, ws in jobs:
        pltpu.make_async_copy(buf, dst, ws).wait()


def finish_kernel(n, from_l_ref, from_r_ref, out_in_ref, out_ref, sem):
    me = lax.axis_index("tp")
    rows, width = out_ref.shape
    piece = width // n
    c = pl.ds(pl.multiple_of(lax.rem(me + 2, n) * piece, piece), piece)
    copies = []
    for i in range(TAIL):
        src = (from_l_ref, from_r_ref)[i % 2].at[i // 2]
        copies.append(pltpu.make_async_copy(src, out_ref.at[pl.ds(rows - (TAIL - i) * UNIT, UNIT), c], sem.at[i]))
    for copy in copies:
        copy.start()
    for copy in copies:
        copy.wait()


def solution(mesh):
    n = mesh.shape["tp"]

    def step(x, w_gate, w_up, w_down):
        rows, din = x.shape
        hidden, width = w_down.shape
        piece = width // n
        rmax = max(BLOCKS)
        ring = pltpu.VMEM((DEPTH, UNIT, piece), BF16)
        dma = pltpu.SemaphoreType.DMA
        rel = jax.ShapeDtypeStruct((TAIL // 2, UNIT, piece), BF16)
        anywhere = pl.BlockSpec(memory_space=pl.ANY)
        y, rel_r, rel_l = pl.pallas_call(
            functools.partial(kernel, n),
            out_shape=(jax.ShapeDtypeStruct((rows, width), BF16), rel, rel),
            in_specs=[anywhere] * 4,
            out_specs=(anywhere,) * 3,
            scratch_shapes=[
                pltpu.VMEM((rmax, din), BF16),
                pltpu.VMEM((WBUF, din, 2 * TN), BF16),
                pltpu.VMEM((rmax, hidden), BF16),
                pltpu.VMEM((DEPTH, n, UNIT, piece), F32),
                ring, ring, ring, ring, ring, ring, ring,
                dma, dma((WBUF,)), dma((DEPTH,)), dma((DEPTH,)), dma((DEPTH,)), dma((DEPTH,)),
                dma((DEPTH + TAIL,)), dma((DEPTH + TAIL,)),
            ],
            compiler_params=pltpu.CompilerParams(
                collective_id=0, has_side_effects=True, vmem_limit_bytes=63 * 2**20),
            cost_estimate=pl.CostEstimate(flops=6 * rows * din * hidden, bytes_accessed=7 * 6 * din * hidden, transcendentals=0),
        )(x, w_gate, w_up, w_down)
        from_l = lax.ppermute(rel_r, "tp", [(i, (i + 1) % n) for i in range(n)])
        from_r = lax.ppermute(rel_l, "tp", [(i, (i - 1) % n) for i in range(n)])
        whole = (rows - TAIL * UNIT) // CHUNK
        out = pl.pallas_call(
            functools.partial(copy_kernel, n),
            out_shape=jax.ShapeDtypeStruct((rows, width), BF16),
            in_specs=[anywhere] * 3,
            out_specs=anywhere,
            scratch_shapes=[
                pltpu.VMEM((whole, CHUNK, width), BF16),
                pltpu.VMEM((TAIL, 3, UNIT, piece), BF16),
                dma((whole,)), dma((whole,)), dma((TAIL, 3)), dma((TAIL, 3)),
            ],
            compiler_params=pltpu.CompilerParams(vmem_limit_bytes=32 * 2**20),
            cost_estimate=pl.CostEstimate(flops=10**10, bytes_accessed=4 * rows * width, transcendentals=0),
        )(y, *(pltpu.with_memory_space_constraint(v, pltpu.HBM) for v in (rel_r, rel_l)))
        vmem = pl.BlockSpec(memory_space=pltpu.VMEM)
        from_l = pltpu.with_memory_space_constraint(from_l, pltpu.VMEM)
        from_r = pltpu.with_memory_space_constraint(from_r, pltpu.VMEM)
        return pl.pallas_call(
            functools.partial(finish_kernel, n),
            out_shape=jax.ShapeDtypeStruct((rows, width), BF16),
            in_specs=[vmem, vmem, anywhere],
            out_specs=anywhere,
            input_output_aliases={2: 0},
            scratch_shapes=[dma((TAIL,))],
        )(from_l, from_r, out)

    return jax.shard_map(
        step,
        mesh=mesh,
        in_specs=(P("dp", None), P(None, "tp"), P(None, "tp"), P("tp", None)),
        out_specs=P("dp", None),
        check_vma=False,
    )
```

time: 475 us -> 450 us (0.947)
  local copies, waits for them, and re-layouts: 21 us -> 0 us
  Pallas kernels: 454 us -> 446 us
    unnamed x1 -> x0, local copies, waits for them, and re-layouts: 21 us -> none
    pallas_call x1 -> x3, Pallas kernels: 454 us -> 446 us  [the longest x1 428 us: step(): pl.pallas_call(functools.partial(kernel, n), out_shape=(jax.ShapeDtypeStr...]
  transfers between devices with their start and end apart: 0 -> 2, of which waited for: 0 -> 0; matrix products, arithmetic and copies ran while one was open for 0% -> 0% of each run, Pallas kernels for 0% -> 4%
where the time goes in v2:
time: 450 us
  Pallas kernels  446 us (99%)
    pallas_call x1, Pallas kernels, step(): pl.pallas_call(functools.partial(kernel, n), out_shape=(jax.ShapeDtypeStr...  428 us
    pallas_call x1, Pallas kernels, step(): pl.pallas_call(functools.partial(copy_kernel, n), out_shape=jax.ShapeDtyp...  16.9 us
  transfers between devices with their start and end apart: 2, of which 0 were waited for; matrix products, arithmetic and copies ran while one was open for 0% of the time, Pallas kernels for 4%

profile of v2, /device:TPU:112, one launch (start us, length us, event | category | flops | bytes accessed | tf_op | source)
XLA Modules:
  0.0 449.7 jit_solution(13564261688553407452)
XLA Ops:
  0.0 428.2 %shard_map.46 = (bf16[2048,6144]{1,0:T(8,128)(2,1)}, bf16[4,64,1536]{2,1,0:T(8,128)(2,1)}, bf16[4,64,1536]{2,1,0:T(8,128)(2,1)}) custom-call(bf16[2048,6144]{1,0:T(8,128)(2,1)} %x_ref.1, bf16[6144,4096]{1,0:T(8,128)(2,1)} %wg_ref.1, bf16[6144,4096]{1,0:T(8,128)(2,1)} %wu_ref.1, bf16[4096,6144]{1,0:T(8,128)(2,1)} %wd_ref.1), custom_call_target="tpu_custom_call" | custom-call | flops 309237645312 | bytes 1056964608 | tf_op jit(solution)/shard_map/pallas_call | solution.py:361
  428.2 1.6 collective-permute-start
  429.8 1.7 collective-permute-start.1
  431.5 16.9 %shard_map.47.out_in_ref = bf16[2048,6144]{1,0:T(8,128)(2,1)} custom-call(bf16[2048,6144]{1,0:T(8,128)(2,1)} %get-tuple-element.10.y_ref, bf16[4,64,1536]{2,1,0:T(8,128)(2,1)} %get-tuple-element.8.rel_r_ref, bf16[4,64,1536]{2,1,0:T(8,128)(2,1)} %get-tuple-element.9.rel_l_ref), custom_call_target="tpu_custom_call" | custom-call | flops 10000000000 | bytes 50331648 | tf_op jit(solution)/shard_map/pallas_call | solution.py:382
  448.4 0.0 collective-permute-done.from_l_ref
  448.5 0.0 collective-permute-done.1.from_r_ref
  448.5 1.2 shard_map.48
Async XLA Ops:
  428.2 20.3 %collective-permute-start = (bf16[4,64,1536]{2,1,0:T(8,128)(2,1)}, bf16[4,64,1536]{2,1,0:T(8,128)(2,1)S(1)}, u32[]{:S(2)}, u32[]{:S(2)}) collective-permute-start(bf16[4,64,1536]{2,1,0:T(8,128)(2,1)} %get-tuple-element.8.rel_r_ref), channel_id=1, source_target_pairs={{0,1},{1,2},{2,3},{3,0},{4,5},{5,6},{6,7},{7,4},{8,9},{9,10},{10,1... | collective-permute-start | bytes 2359304 | tf_op jit(solution)/shard_map/ppermute | solution.py:379
  429.8 18.7 %collective-permute-start.1 = (bf16[4,64,1536]{2,1,0:T(8,128)(2,1)}, bf16[4,64,1536]{2,1,0:T(8,128)(2,1)S(1)}, u32[]{:S(2)}, u32[]{:S(2)}) collective-permute-start(bf16[4,64,1536]{2,1,0:T(8,128)(2,1)} %get-tuple-element.9.rel_l_ref), channel_id=1, source_target_pairs={{0,3},{1,0},{2,1},{3,2},{4,7},{5,4},{6,5},{7,6},{8,11},{9,8},{10,9... | collective-permute-start | bytes 2359304 | tf_op jit(solution)/shard_map/ppermute | solution.py:380

commit v3 on v2

--- a/solution.py
+++ b/solution.py
@@ -10,20 +10,22 @@
 MESH = pl.DeviceIdType.MESH
 F32, BF16 = jnp.float32, jnp.bfloat16
 
-BLOCKS = (256, 256, 320, 320, 320, 320, 256)
-UNIT = 64
-DEPTH = 10
+BLOCKS = (128, 128, 128, 128, 128, 128, 128, 128, 128, 128, 128, 128, 128, 128, 128, 128)
+UNIT = 32
+LAG = 8
+MATE = 4
+DEPTH = 20
 WBUF = 3
 TN = 256
-TD = 768
-TAIL = 8
+TD = 1536
+TAIL = 16
 CHUNK = 128
 
 SCHEDULE = {
-    "pair": [21, 22, 23, 24, 47, 48, 49, 50, 69, 70, 71, 72, 73, 94, 96, 97, 98, 99, 119, 120, 121, 122, 123, 145, 146, 147, 148, 149, 169, 170, 171, 172],
-    "own": [28, 29, 31, 32, 53, 54, 55, 56, 76, 77, 78, 79, 80, 101, 104, 105, 106, 107, 128, 129, 130, 131, 132, 156, 160, 161, 162, 163, 176, 177, 178, 179],
-    "relay": [33, 35, 37, 40, 57, 59, 60, 62, 81, 83, 85, 86, 88, 107, 109, 111, 113, 114, 134, 135, 137, 139, 140, 163, 168, 173, 174, 175, 180, 181, 182, 183],
-    "free": [35, 37, 40, 57, 59, 60, 62, 81, 83, 85, 86, 88, 107, 109, 111, 113, 114, 134, 135, 137, 139, 140, 163, 168, 173, 174, 175, 180, 181, 182, 183, 184],
+    "pair": [12, 13, 24, 25, 36, 37, 48, 49, 60, 61, 72, 73, 84, 85, 97, 98, 109, 110, 120, 121, 134, 135, 144, 145, 156, 157, 169, 170, 182, 183, 192, 193],
+    "own": [16, 17, 28, 30, 40, 42, 53, 55, 65, 67, 77, 80, 90, 92, 102, 104, 115, 117, 127, 128, 139, 141, 152, 153, 164, 165, 175, 176, 186, 187, 194, 195],
+    "relay": [20, 24, 32, 36, 45, 48, 57, 60, 69, 72, 82, 84, 94, 97, 106, 109, 119, 123, 131, 134, 143, 147, 155, 160, 168, 172, 179, 182, 190, 192, 196, 197],
+    "free": [20, 24, 32, 36, 45, 48, 57, 60, 69, 72, 82, 84, 94, 97, 106, 109, 119, 123, 131, 134, 143, 147, 155, 160, 168, 172, 179, 182, 190, 192, 196, 197],
 }
 EVENTS = tuple(SCHEDULE)
 
@@ -38,10 +40,13 @@
 
 def kernel(n, x_ref, wg_ref, wu_ref, wd_ref, y_ref, rel_r_ref, rel_l_ref, xv, wv, hv, hold,
            opp_s, dir_s, sum_s, own_s, opp_r, dir_r, sum_r,
-           x_sem, w_sem, out_sem, opp_rs, own_rs, ag_rs, re_ss, re_rs):
+           mate_s, mate_r,
+           x_sem, px_ss, px_rs, w_sem, out_sem, opp_rs, own_rs, ag_rs, re_ss, re_rs, mate_ss, mate_rs):
     me = lax.axis_index("tp")
+    core = lax.rem(lax.axis_index("dp"), 2)
+    mate = lax.axis_index("dp") + 1 - 2 * core
     rows, depth_in = x_ref.shape
-    hidden, width = wd_ref.shape
+    hidden, width = wd_ref.shape[0] // 2, wd_ref.shape[1]
     piece = width // n
     nu = rows // UNIT
     kept = nu - TAIL
@@ -71,27 +76,27 @@
         return pl.ds(pl.multiple_of(s * UNIT, UNIT), UNIT)
 
     def gu_copies(t, slot):
-        c = pl.ds(pl.multiple_of(t * TN, TN), TN)
+        c = pl.ds(pl.multiple_of(core * hidden + t * TN, TN), TN)
         return (pltpu.make_async_copy(wg_ref.at[:, c], wv.at[slot, :, 0:TN], w_sem.at[slot]),
                 pltpu.make_async_copy(wu_ref.at[:, c], wv.at[slot, :, TN:2 * TN], w_sem.at[slot]))
 
-    side, half = TD - 2 * TN, hidden // 2
+    third = 2 * TN
 
     def dn_copies(t, slot):
         p, j = t // per_piece, lax.rem(t, per_piece)
         c = at(pick(p, (2, 1, 3, 0))) * piece + j * TD
-        main = pl.ds(pl.multiple_of(c, TN), 2 * TN)
-        rest = pl.ds(pl.multiple_of(c + 2 * TN, TN), side)
-        return (pltpu.make_async_copy(wd_ref.at[:, main], wv.at[slot, 0:hidden, :], w_sem.at[slot]),
-                pltpu.make_async_copy(wd_ref.at[0:half, rest], wv.at[slot, hidden:hidden + half, 0:side], w_sem.at[slot]),
-                pltpu.make_async_copy(wd_ref.at[half:hidden, rest], wv.at[slot, hidden:hidden + half, side:2 * side], w_sem.at[slot]))
+        r = pl.ds(pl.multiple_of(core * hidden, TN), hidden)
+        return [pltpu.make_async_copy(wd_ref.at[r, pl.ds(pl.multiple_of(c + i * third, TN), third)],
+                                      wv.at[slot, i * hidden:(i + 1) * hidden, :], w_sem.at[slot])
+                for i in range(TD // third)]
 
     def start_dn(t, slot):
         for c in dn_copies(t, slot):
             c.start()
 
-    def tile_wait(slot):
-        pltpu.make_async_copy(wv.at[slot], wv.at[slot], w_sem.at[slot]).wait()
+    def tile_wait(slot, depth):
+        tile = wv.at[slot, 0:depth, :]
+        pltpu.make_async_copy(tile, tile, w_sem.at[slot]).wait()
 
     def start_gu(t, slot):
         for c in gu_copies(t, slot):
@@ -100,6 +105,17 @@
     def x_copy(b, r):
         return pltpu.make_async_copy(x_ref.at[pl.ds(pl.multiple_of(pick(b, row0), UNIT), r), :], xv.at[pl.ds(0, r), :], x_sem)
 
+    def push_copy(b, r):
+        return pltpu.make_async_remote_copy(
+            src_ref=x_ref.at[pl.ds(pl.multiple_of(pick(b, row0), UNIT), r), :], dst_ref=xv.at[pl.ds(r, r), :],
+            send_sem=px_ss, recv_sem=px_rs, device_id={"dp": mate}, device_id_type=MESH)
+
+    def mate_copy(b, t, r):
+        q = lax.rem(b * dn_steps + t, MATE)
+        return pltpu.make_async_remote_copy(
+            src_ref=mate_s.at[q, pl.ds(0, r), :], dst_ref=mate_r.at[q, pl.ds(0, r), :],
+            send_sem=mate_ss.at[q], recv_sem=mate_rs.at[q], device_id={"dp": mate}, device_id_type=MESH)
+
     def opp_copy(s, slot, par, c):
         return remote(opp_s.at[slot, :, c], opp_r.at[slot, :, c], out_sem.at[slot], opp_rs.at[slot], at(1 + 2 * par))
 
@@ -118,7 +134,7 @@
 
     def relay_copy(s, par):
         view = y_ref.at[unit_rows(s), cols(at(3 - 2 * par))]
-        k = lax.rem(s, DEPTH + TAIL)
+        k = lax.rem(s, DEPTH + LAG)
         return remote(view, view, re_ss.at[k], re_rs.at[k], at(1 + 2 * par))
 
     def loc_copy(s, slot):
@@ -130,43 +146,49 @@
         size = hold.at[0, 0:pieces // 2]
         pltpu.make_async_copy(size, size, sem).wait()
 
-    def pair(s):
-        slot, par = lax.rem(s, DEPTH), lax.rem(s, 2)
-        opp_copy(s, slot, par, whole).wait_recv()
-        sum_s[slot] = (hold[slot, 1 + par] + opp_r[slot].astype(F32)).astype(BF16)
-        sum_copy(s, slot, par).start()
-
-    def own(s):
-        slot, par = lax.rem(s, DEPTH), lax.rem(s, 2)
-        arrived(own_rs.at[slot], 2)
-        own_s[slot] = (hold[slot, 3] + sum_r[slot].astype(F32) + dir_r[slot].astype(F32)).astype(BF16)
-        for side in (0, 1):
-            keep = (s >= kept) & (par == side)
-
-            @pl.when(keep)
-            def _(side=side):
-                keep_copy(s, slot, side).start()
-
-            @pl.when(jnp.logical_not(keep))
-            def _(side=side):
-                own_copy(s, slot, side).start()
-        loc_copy(s, slot).start()
-
-    def relay(s):
-        slot, par = lax.rem(s, DEPTH), lax.rem(s, 2)
-        arrived(ag_rs.at[slot], 2)
-
-        @pl.when(s < kept)
+    def duo(k):
+        return [(2 * k + par, lax.rem(2 * k + par, DEPTH), par) for par in (0, 1)]
+
+    def pair(k):
+        for s, slot, par in duo(k):
+            opp_copy(s, slot, par, whole).wait_recv()
+            sum_s[slot] = (hold[slot, 1 + par] + opp_r[slot].astype(F32)).astype(BF16)
+            sum_copy(s, slot, par).start()
+
+    def own(k):
+        for s, slot, par in duo(k):
+            arrived(own_rs.at[slot], 2)
+            own_s[slot] = (hold[slot, 3] + sum_r[slot].astype(F32) + dir_r[slot].astype(F32)).astype(BF16)
+            own_copy(s, slot, 1 - par).start()
+            loc_copy(s, slot).start()
+
+        @pl.when(2 * k < kept)
         def _():
-            relay_copy(s, par).start()
-
-    def free(s):
-        slot, par = lax.rem(s, DEPTH), lax.rem(s, 2)
-        arrived(out_sem.at[slot], 6)
-
-        @pl.when((s >= TAIL) & (s < kept + TAIL))
+            for s, slot, par in duo(k):
+                own_copy(s, slot, par).start()
+
+        @pl.when(2 * k >= kept)
         def _():
-            relay_copy(s - TAIL, par).wait()
+            for s, slot, par in duo(k):
+                keep_copy(s, slot, par).start()
+
+    def relay(k):
+        for s, slot, par in duo(k):
+            arrived(ag_rs.at[slot], 2)
+
+        @pl.when(2 * k < kept)
+        def _():
+            for s, slot, par in duo(k):
+                relay_copy(s, par).start()
+
+    def free(k):
+        for s, slot, par in duo(k):
+            arrived(out_sem.at[slot], 6)
+
+        @pl.when((2 * k >= LAG) & (2 * k < kept + LAG))
+        def _():
+            for s, slot, par in duo(k):
+                relay_copy(s - LAG, par).wait()
 
     actions = {"pair": pair, "own": own, "relay": relay, "free": free}
 
@@ -185,15 +207,33 @@
     def state(b):
         return {e: pick(b, masks[e]) for e in EVENTS}, b * steps
 
-    def gu_phase(b, r, exchange=True):
+    def gu_phase(b, r):
         mask, base = state(b)
         x_copy(b, r).wait()
-        if not exchange:
-            start_gu(jnp.int32(1), jnp.int32(1))
+
+        def hidden_rows(lo, hi, t, slot):
+            xb = xv[lo:hi, :]
+            gate = jnp.dot(xb, wv[slot, :, 0:TN], preferred_element_type=F32)
+            up = jnp.dot(xb, wv[slot, :, TN:2 * TN], preferred_element_type=F32)
+            hv[lo:hi, pl.ds(pl.multiple_of(t * TN, TN), TN)] = (jax.nn.silu(gate) * up).astype(BF16)
+
+        @pl.when(b > 0)
+        def _():
+            push_copy(b, r).wait()
+
+        if r == BLOCKS[0]:
+            @pl.when(b == 0)
+            def _():
+                start_gu(jnp.int32(1), jnp.int32(1))
+                tile_wait(jnp.int32(0), depth_in)
+                start_gu(jnp.int32(2), jnp.int32(2))
+                hidden_rows(0, r, jnp.int32(0), jnp.int32(0))
+                push_copy(b, r).wait()
+                hidden_rows(r, 2 * r, jnp.int32(0), jnp.int32(0))
 
         def gu_step(t, done):
             slot = lax.rem(base + t, WBUF)
-            tile_wait(slot)
+            tile_wait(slot, depth_in)
             ahead = t + WBUF - 1
             later = lax.rem(base + ahead, WBUF)
 
@@ -205,75 +245,69 @@
             def _():
                 start_dn(ahead - gu_steps, later)
 
-            xb = xv[0:r, :]
-            gate = jnp.dot(xb, wv[slot, :, 0:TN], preferred_element_type=F32)
-            up = jnp.dot(xb, wv[slot, :, TN:2 * TN], preferred_element_type=F32)
-            hv[0:r, pl.ds(pl.multiple_of(t * TN, TN), TN)] = (jax.nn.silu(gate) * up).astype(BF16)
-            return events(t, mask, done) if exchange else done
-
-        lax.fori_loop(0, gu_steps, gu_step, tuple(pick(b, starts[e]) for e in EVENTS))
+            hidden_rows(0, 2 * r, t, slot)
+
+            @pl.when((t == 0) & (b > 0))
+            def _():
+                switch(b - 1, lambda b, r: merge(b, dn_steps - 1, r))
+
+            return events(t, mask, done)
+
+        lax.fori_loop(jnp.where(b == 0, 1, 0), gu_steps, gu_step, tuple(pick(b, starts[e]) for e in EVENTS))
+
+    def merge(b, t, r):
+        first = pick(b, [v // UNIT for v in row0])
+        q = lax.rem(b * dn_steps + t, MATE)
+        mate_copy(b, t, r).wait()
+        for k in range(r // UNIT):
+            s, par = first + k, k % 2
+            slot = lax.rem(s, DEPTH)
+            both = hold[slot, t] + mate_r[q, k * UNIT:(k + 1) * UNIT, :].astype(F32)
+            if t == 0:
+                opp_s[slot] = both.astype(BF16)
+                opp_copy(s, slot, par, whole).start()
+            elif t == 2 - par:
+                dir_s[slot] = both.astype(BF16)
+                dir_copy(s, slot, par, whole).start()
+            else:
+                hold[slot, t] = both
 
     def dn_phase(b, r):
         units = r // UNIT
         first = pick(b, [v // UNIT for v in row0])
         mask, base = state(b)
-        for r2 in sorted(set(BLOCKS)):
-            @pl.when(pick(b + 1, [v == r2 for v in BLOCKS]) == 1)
-            def _(r2=r2):
-                x_copy(b + 1, r2).start()
-
-        def dn_step(t, done):
+
+        done = tuple(pick(b, mid[e]) for e in EVENTS)
+        for t in range(dn_steps):
             g = base + gu_steps + t
             slot = lax.rem(g, WBUF)
-            tile_wait(slot)
+            tile_wait(slot, dn_steps // n * hidden * TD // (2 * TN))
             ahead = t + WBUF - 1
             later = lax.rem(g + WBUF - 1, WBUF)
-
-            @pl.when(ahead < dn_steps)
-            def _():
-                start_dn(ahead, later)
-
-            @pl.when((ahead >= dn_steps) & (b + 1 < nb))
-            def _():
-                start_gu(ahead - dn_steps, later)
-
-            p, j = t // per_piece, lax.rem(t, per_piece)
-            c = pl.ds(pl.multiple_of(j * TD, TD), TD)
-            term = jnp.dot(hv[0:r, :], wv[slot, 0:hidden, :], preferred_element_type=F32)
-            rest = (jnp.dot(hv[0:r, 0:half], wv[slot, hidden:hidden + half, 0:side], preferred_element_type=F32)
-                    + jnp.dot(hv[0:r, half:hidden], wv[slot, hidden:hidden + half, side:2 * side], preferred_element_type=F32))
-            c0 = pl.ds(pl.multiple_of(j * TD, TN), 2 * TN)
-            c1 = pl.ds(pl.multiple_of(j * TD + 2 * TN, TN), side)
-            for k in range(units):
-                hold[lax.rem(first + k, DEPTH), p, :, c0] = term[k * UNIT:(k + 1) * UNIT, :]
-                hold[lax.rem(first + k, DEPTH), p, :, c1] = rest[k * UNIT:(k + 1) * UNIT, :]
-
-            @pl.when(p == 0)
-            def _():
-                def send(k, _):
-                    s = first + k
-                    slot, par = lax.rem(s, DEPTH), lax.rem(s, 2)
-                    opp_s[slot, :, c] = hold[slot, 0, :, c].astype(BF16)
-                    opp_copy(s, slot, par, c).start()
-                    return 0
-                lax.fori_loop(0, units, send, 0)
-
-            @pl.when((p == 1) | (p == 2))
-            def _():
-                def send(k, _):
-                    s = first + k
-                    slot, par = lax.rem(s, DEPTH), lax.rem(s, 2)
-
-                    @pl.when(p == 2 - par)
-                    def _():
-                        dir_s[slot, :, c] = hold[slot, p, :, c].astype(BF16)
-                        dir_copy(s, slot, par, c).start()
-                    return 0
-                lax.fori_loop(0, units, send, 0)
-
-            return events(gu_steps + t, mask, done)
-
-        lax.fori_loop(0, dn_steps, dn_step, tuple(pick(b, mid[e]) for e in EVENTS))
+            if ahead < dn_steps:
+                start_dn(jnp.int32(ahead), later)
+            else:
+                @pl.when(b + 1 < nb)
+                def _(ahead=ahead, later=later):
+                    start_gu(jnp.int32(ahead - dn_steps), later)
+
+            q = lax.rem(b * dn_steps + t, MATE)
+            for i in range(TD // third):
+                term = jnp.dot(hv[0:2 * r, :], wv[slot, i * hidden:(i + 1) * hidden, :], preferred_element_type=F32)
+                c = slice(i * third, (i + 1) * third)
+                for k in range(units):
+                    hold[lax.rem(first + k, DEPTH), t, :, c] = term[k * UNIT:(k + 1) * UNIT, :]
+                mate_s[q, 0:r, c] = term[r:2 * r, :].astype(BF16)
+            mate_copy(b, t, r).start()
+            if t > 0:
+                merge(b, t - 1, r)
+            if t == 1:
+                for r2 in sorted(set(BLOCKS)):
+                    @pl.when(pick(b + 1, [v == r2 for v in BLOCKS]) == 1)
+                    def _(r2=r2):
+                        x_copy(b + 1, r2).start()
+                        push_copy(b + 1, r2).start()
+            done = events(jnp.int32(gu_steps + t), mask, done)
 
     def switch(b, phase):
         for r in sorted(set(BLOCKS)):
@@ -281,20 +315,21 @@
             def _(r=r):
                 phase(b, r)
 
-    barrier = pltpu.get_barrier_semaphore()
-    for offset in (1, n - 1):
-        pl.semaphore_signal(barrier, inc=1, device_id={"tp": at(offset)}, device_id_type=MESH)
     x_copy(jnp.int32(0), BLOCKS[0]).start()
     start_gu(jnp.int32(0), jnp.int32(0))
-    gu_phase(jnp.int32(0), BLOCKS[0], exchange=False)
-    pl.semaphore_wait(barrier, 2)
+    barrier = pltpu.get_barrier_semaphore()
+    for other in ({"tp": at(1)}, {"tp": at(n - 1)}, {"dp": mate}):
+        pl.semaphore_signal(barrier, inc=1, device_id=other, device_id_type=MESH)
+    pl.semaphore_wait(barrier, 3)
+    push_copy(jnp.int32(0), BLOCKS[0]).start()
 
     def outer(b, _):
+        switch(b, gu_phase)
         switch(b, dn_phase)
-        switch(b + 1, gu_phase)
         return 0
 
     lax.fori_loop(0, nb, outer, 0)
+    merge(jnp.int32(nb - 1), dn_steps - 1, BLOCKS[-1])
 
     def tail(g, done):
         b = g // steps
@@ -364,13 +399,14 @@
             in_specs=[anywhere] * 4,
             out_specs=(anywhere,) * 3,
             scratch_shapes=[
-                pltpu.VMEM((rmax, din), BF16),
+                pltpu.VMEM((2 * rmax, din), BF16),
                 pltpu.VMEM((WBUF, din, 2 * TN), BF16),
-                pltpu.VMEM((rmax, hidden), BF16),
+                pltpu.VMEM((2 * rmax, hidden // 2), BF16),
                 pltpu.VMEM((DEPTH, n, UNIT, piece), F32),
                 ring, ring, ring, ring, ring, ring, ring,
-                dma, dma((WBUF,)), dma((DEPTH,)), dma((DEPTH,)), dma((DEPTH,)), dma((DEPTH,)),
-                dma((DEPTH + TAIL,)), dma((DEPTH + TAIL,)),
+                pltpu.VMEM((MATE, rmax, TD), BF16), pltpu.VMEM((MATE, rmax, TD), BF16),
+                dma, dma, dma, dma((WBUF,)), dma((DEPTH,)), dma((DEPTH,)), dma((DEPTH,)), dma((DEPTH,)),
+                dma((DEPTH + LAG,)), dma((DEPTH + LAG,)), dma((MATE,)), dma((MATE,)),
             ],
             compiler_params=pltpu.CompilerParams(
                 collective_id=0, has_side_effects=True, vmem_limit_bytes=63 * 2**20),

time: 450 us -> 443 us (0.984)
  Pallas kernels: 446 us -> 439 us
    pallas_call x1, Pallas kernels: 428 us -> 421 us  [step(): pl.pallas_call(functools.partial(kernel, n), out_shape=(jax.ShapeDtypeStr...]
where the time goes in v3:
time: 443 us
  Pallas kernels  439 us (99%)
    pallas_call x1, Pallas kernels, step(): pl.pallas_call(functools.partial(kernel, n), out_shape=(jax.ShapeDtypeStr...  421 us
    pallas_call x1, Pallas kernels, step(): pl.pallas_call(functools.partial(copy_kernel, n), out_shape=jax.ShapeDtyp...  17 us
  transfers between devices with their start and end apart: 2, of which 0 were waited for; matrix products, arithmetic and copies ran while one was open for 0% of the time, Pallas kernels for 4%

profile of v3, /device:TPU:112, one launch (start us, length us, event | category | flops | bytes accessed | tf_op | source)
XLA Modules:
  0.0 442.5 jit_solution(13330305996238350056)
XLA Ops:
  0.0 420.9 %shard_map.46 = (bf16[2048,6144]{1,0:T(8,128)(2,1)}, bf16[8,32,1536]{2,1,0:T(8,128)(2,1)}, bf16[8,32,1536]{2,1,0:T(8,128)(2,1)}) custom-call(bf16[2048,6144]{1,0:T(8,128)(2,1)} %x_ref.1, bf16[6144,4096]{1,0:T(8,128)(2,1)} %wg_ref.1, bf16[6144,4096]{1,0:T(8,128)(2,1)} %wu_ref.1, bf16[4096,6144]{1,0:T(8,128)(2,1)} %wd_ref.1), custom_call_target="tpu_custom_call" | custom-call | flops 309237645312 | bytes 1056964608 | tf_op jit(solution)/shard_map/pallas_call | solution.py:396
  420.9 0.4 collective-permute-start
  421.3 2.9 collective-permute-start.1
  424.2 17.0 %shard_map.47.out_in_ref = bf16[2048,6144]{1,0:T(8,128)(2,1)} custom-call(bf16[2048,6144]{1,0:T(8,128)(2,1)} %get-tuple-element.10.y_ref, bf16[8,32,1536]{2,1,0:T(8,128)(2,1)} %get-tuple-element.8.rel_r_ref, bf16[8,32,1536]{2,1,0:T(8,128)(2,1)} %get-tuple-element.9.rel_l_ref), custom_call_target="tpu_custom_call" | custom-call | flops 10000000000 | bytes 50331648 | tf_op jit(solution)/shard_map/pallas_call | solution.py:418
  441.2 0.0 collective-permute-done.from_l_ref
  441.2 0.0 collective-permute-done.1.from_r_ref
  441.3 1.3 shard_map.48
Async XLA Ops:
  420.9 20.3 %collective-permute-start = (bf16[8,32,1536]{2,1,0:T(8,128)(2,1)}, bf16[8,32,1536]{2,1,0:T(8,128)(2,1)S(1)}, u32[]{:S(2)}, u32[]{:S(2)}) collective-permute-start(bf16[8,32,1536]{2,1,0:T(8,128)(2,1)} %get-tuple-element.8.rel_r_ref), channel_id=1, source_target_pairs={{0,1},{1,2},{2,3},{3,0},{4,5},{5,6},{6,7},{7,4},{8,9},{9,10},{10,1... | collective-permute-start | bytes 2359304 | tf_op jit(solution)/shard_map/ppermute | solution.py:415
  421.3 19.9 %collective-permute-start.1 = (bf16[8,32,1536]{2,1,0:T(8,128)(2,1)}, bf16[8,32,1536]{2,1,0:T(8,128)(2,1)S(1)}, u32[]{:S(2)}, u32[]{:S(2)}) collective-permute-start(bf16[8,32,1536]{2,1,0:T(8,128)(2,1)} %get-tuple-element.9.rel_l_ref), channel_id=1, source_target_pairs={{0,3},{1,0},{2,1},{3,2},{4,7},{5,4},{6,5},{7,6},{8,11},{9,8},{10,9... | collective-permute-start | bytes 2359304 | tf_op jit(solution)/shard_map/ppermute | solution.py:416

commit v4 on v3

--- a/solution.py
+++ b/solution.py
@@ -10,7 +10,7 @@
 MESH = pl.DeviceIdType.MESH
 F32, BF16 = jnp.float32, jnp.bfloat16
 
-BLOCKS = (128, 128, 128, 128, 128, 128, 128, 128, 128, 128, 128, 128, 128, 128, 128, 128)
+BLOCKS = (128, 128, 128, 128, 128, 128, 128, 128, 128, 128, 128, 192, 192, 128, 128)
 UNIT = 32
 LAG = 8
 MATE = 4
@@ -22,10 +22,10 @@
 CHUNK = 128
 
 SCHEDULE = {
-    "pair": [12, 13, 24, 25, 36, 37, 48, 49, 60, 61, 72, 73, 84, 85, 97, 98, 109, 110, 120, 121, 134, 135, 144, 145, 156, 157, 169, 170, 182, 183, 192, 193],
-    "own": [16, 17, 28, 30, 40, 42, 53, 55, 65, 67, 77, 80, 90, 92, 102, 104, 115, 117, 127, 128, 139, 141, 152, 153, 164, 165, 175, 176, 186, 187, 194, 195],
-    "relay": [20, 24, 32, 36, 45, 48, 57, 60, 69, 72, 82, 84, 94, 97, 106, 109, 119, 123, 131, 134, 143, 147, 155, 160, 168, 172, 179, 182, 190, 192, 196, 197],
-    "free": [20, 24, 32, 36, 45, 48, 57, 60, 69, 72, 82, 84, 94, 97, 106, 109, 119, 123, 131, 134, 143, 147, 155, 160, 168, 172, 179, 182, 190, 192, 196, 197],
+    "pair": [12, 13, 24, 25, 36, 37, 48, 49, 60, 61, 72, 73, 84, 85, 97, 98, 109, 110, 120, 121, 133, 134, 143, 144, 145, 156, 157, 158, 171, 172, 180, 181],
+    "own": [16, 17, 28, 30, 40, 42, 53, 55, 65, 67, 77, 80, 90, 92, 102, 104, 115, 117, 127, 128, 137, 138, 147, 149, 150, 162, 163, 164, 175, 176, 182, 183],
+    "relay": [20, 24, 32, 36, 45, 48, 57, 60, 69, 72, 82, 84, 94, 97, 106, 109, 119, 123, 131, 133, 140, 143, 151, 152, 156, 166, 168, 171, 179, 180, 184, 185],
+    "free": [20, 24, 32, 36, 45, 48, 57, 60, 69, 72, 82, 84, 94, 97, 106, 109, 119, 123, 131, 133, 140, 143, 151, 152, 156, 166, 168, 171, 179, 180, 184, 185],
 }
 EVENTS = tuple(SCHEDULE)
 
@@ -117,47 +117,47 @@
             send_sem=mate_ss.at[q], recv_sem=mate_rs.at[q], device_id={"dp": mate}, device_id_type=MESH)
 
     def opp_copy(s, slot, par, c):
-        return remote(opp_s.at[slot, :, c], opp_r.at[slot, :, c], out_sem.at[slot], opp_rs.at[slot], at(1 + 2 * par))
+        return remote(opp_s.at[slot, :, c], opp_r.at[slot, :, c], out_sem.at[slot // 2], opp_rs.at[slot // 2], at(1 + 2 * par))
 
     def dir_copy(s, slot, par, c):
-        return remote(dir_s.at[slot, :, c], dir_r.at[slot, :, c], out_sem.at[slot], own_rs.at[slot], at(3 - 2 * par))
+        return remote(dir_s.at[slot, :, c], dir_r.at[slot, :, c], out_sem.at[slot // 2], own_rs.at[slot // 2], at(3 - 2 * par))
 
     def sum_copy(s, slot, par):
-        return remote(sum_s.at[slot], sum_r.at[slot], out_sem.at[slot], own_rs.at[slot], at(1 + 2 * par))
+        return remote(sum_s.at[slot], sum_r.at[slot], out_sem.at[slot // 2], own_rs.at[slot // 2], at(1 + 2 * par))
 
     def own_copy(s, slot, side):
-        return remote(own_s.at[slot], y_ref.at[unit_rows(s), cols(me)], out_sem.at[slot], ag_rs.at[slot], at(1 + 2 * side))
+        return remote(own_s.at[slot], y_ref.at[unit_rows(s), cols(me)], out_sem.at[slot // 2], ag_rs.at[slot // 2], at(1 + 2 * side))
 
     def keep_copy(s, slot, side):
         rel = (rel_r_ref, rel_l_ref)[side].at[(s - kept) // 2]
-        return remote(own_s.at[slot], rel, out_sem.at[slot], ag_rs.at[slot], at(1 + 2 * side))
+        return remote(own_s.at[slot], rel, out_sem.at[slot // 2], ag_rs.at[slot // 2], at(1 + 2 * side))
 
     def relay_copy(s, par):
         view = y_ref.at[unit_rows(s), cols(at(3 - 2 * par))]
-        k = lax.rem(s, DEPTH + LAG)
+        k = lax.rem(s, DEPTH + LAG) // 2
         return remote(view, view, re_ss.at[k], re_rs.at[k], at(1 + 2 * par))
 
     def loc_copy(s, slot):
-        return pltpu.make_async_copy(own_s.at[slot], y_ref.at[unit_rows(s), cols(me)], out_sem.at[slot])
+        return pltpu.make_async_copy(own_s.at[slot], y_ref.at[unit_rows(s), cols(me)], out_sem.at[slot // 2])
 
     whole = pl.ds(0, piece)
 
-    def arrived(sem, pieces):
-        size = hold.at[0, 0:pieces // 2]
-        pltpu.make_async_copy(size, size, sem).wait()
+    def arrived(sem, k, pieces):
+        size = hold.at[0:pieces // 2, 0]
+        pltpu.make_async_copy(size, size, sem.at[lax.rem(k, DEPTH // 2)]).wait()
 
     def duo(k):
         return [(2 * k + par, lax.rem(2 * k + par, DEPTH), par) for par in (0, 1)]
 
     def pair(k):
+        arrived(opp_rs, k, 2)
         for s, slot, par in duo(k):
-            opp_copy(s, slot, par, whole).wait_recv()
             sum_s[slot] = (hold[slot, 1 + par] + opp_r[slot].astype(F32)).astype(BF16)
             sum_copy(s, slot, par).start()
 
     def own(k):
+        arrived(own_rs, k, 4)
         for s, slot, par in duo(k):
-            arrived(own_rs.at[slot], 2)
             own_s[slot] = (hold[slot, 3] + sum_r[slot].astype(F32) + dir_r[slot].astype(F32)).astype(BF16)
             own_copy(s, slot, 1 - par).start()
             loc_copy(s, slot).start()
@@ -173,8 +173,7 @@
                 keep_copy(s, slot, par).start()
 
     def relay(k):
-        for s, slot, par in duo(k):
-            arrived(ag_rs.at[slot], 2)
+        arrived(ag_rs, k, 4)
 
         @pl.when(2 * k < kept)
         def _():
@@ -182,27 +181,27 @@
                 relay_copy(s, par).start()
 
     def free(k):
-        for s, slot, par in duo(k):
-            arrived(out_sem.at[slot], 6)
+        arrived(out_sem, k, 12)
 
         @pl.when((2 * k >= LAG) & (2 * k < kept + LAG))
         def _():
-            for s, slot, par in duo(k):
-                relay_copy(s - LAG, par).wait()
+            i = lax.rem(2 * k - LAG, DEPTH + LAG) // 2
+            for sem in (re_ss, re_rs):
+                pltpu.make_async_copy(hold.at[0, 0], hold.at[0, 0], sem.at[i]).wait()
 
     actions = {"pair": pair, "own": own, "relay": relay, "free": free}
 
     def events(t, mask, done):
-        out = []
-        for e in EVENTS:
-            hit = lax.shift_right_logical(mask[e], t) & 1
-
-            @pl.when(hit == 1)
-            def _(e=e, c=done[len(out)]):
-                actions[e](c)
-
-            out.append(done[len(out)] + hit)
-        return tuple(out)
+        hits = [lax.shift_right_logical(mask[e], t) & 1 for e in EVENTS]
+
+        @pl.when(sum(hits) > 0)
+        def _():
+            for e, hit, c in zip(EVENTS, hits, done):
+                @pl.when(hit == 1)
+                def _(e=e, c=c):
+                    actions[e](c)
+
+        return tuple(c + hit for c, hit in zip(done, hits))
 
     def state(b):
         return {e: pick(b, masks[e]) for e in EVENTS}, b * steps
@@ -277,19 +276,20 @@
         first = pick(b, [v // UNIT for v in row0])
         mask, base = state(b)
 
-        done = tuple(pick(b, mid[e]) for e in EVENTS)
-        for t in range(dn_steps):
+        def dn_step(t, done):
             g = base + gu_steps + t
             slot = lax.rem(g, WBUF)
             tile_wait(slot, dn_steps // n * hidden * TD // (2 * TN))
             ahead = t + WBUF - 1
             later = lax.rem(g + WBUF - 1, WBUF)
-            if ahead < dn_steps:
-                start_dn(jnp.int32(ahead), later)
-            else:
-                @pl.when(b + 1 < nb)
-                def _(ahead=ahead, later=later):
-                    start_gu(jnp.int32(ahead - dn_steps), later)
+
+            @pl.when(ahead < dn_steps)
+            def _():
+                start_dn(ahead, later)
+
+            @pl.when((ahead >= dn_steps) & (b + 1 < nb))
+            def _():
+                start_gu(ahead - dn_steps, later)
 
             q = lax.rem(b * dn_steps + t, MATE)
             for i in range(TD // third):
@@ -299,15 +299,19 @@
                     hold[lax.rem(first + k, DEPTH), t, :, c] = term[k * UNIT:(k + 1) * UNIT, :]
                 mate_s[q, 0:r, c] = term[r:2 * r, :].astype(BF16)
             mate_copy(b, t, r).start()
-            if t > 0:
-                merge(b, t - 1, r)
-            if t == 1:
-                for r2 in sorted(set(BLOCKS)):
-                    @pl.when(pick(b + 1, [v == r2 for v in BLOCKS]) == 1)
-                    def _(r2=r2):
-                        x_copy(b + 1, r2).start()
-                        push_copy(b + 1, r2).start()
-            done = events(jnp.int32(gu_steps + t), mask, done)
+            for done_tile in range(dn_steps - 1):
+                @pl.when(t == done_tile + 1)
+                def _(done_tile=done_tile):
+                    merge(b, done_tile, r)
+                    if done_tile == 0:
+                        for r2 in sorted(set(BLOCKS)):
+                            @pl.when(pick(b + 1, [v == r2 for v in BLOCKS]) == 1)
+                            def _(r2=r2):
+                                x_copy(b + 1, r2).start()
+                                push_copy(b + 1, r2).start()
+            return events(gu_steps + t, mask, done)
+
+        lax.fori_loop(0, dn_steps, dn_step, tuple(pick(b, mid[e]) for e in EVENTS))
 
     def switch(b, phase):
         for r in sorted(set(BLOCKS)):
@@ -405,8 +409,8 @@
                 pltpu.VMEM((DEPTH, n, UNIT, piece), F32),
                 ring, ring, ring, ring, ring, ring, ring,
                 pltpu.VMEM((MATE, rmax, TD), BF16), pltpu.VMEM((MATE, rmax, TD), BF16),
-                dma, dma, dma, dma((WBUF,)), dma((DEPTH,)), dma((DEPTH,)), dma((DEPTH,)), dma((DEPTH,)),
-                dma((DEPTH + LAG,)), dma((DEPTH + LAG,)), dma((MATE,)), dma((MATE,)),
+                dma, dma, dma, dma((WBUF,)), dma((DEPTH // 2,)), dma((DEPTH // 2,)), dma((DEPTH // 2,)), dma((DEPTH // 2,)),
+                dma(((DEPTH + LAG) // 2,)), dma(((DEPTH + LAG) // 2,)), dma((MATE + 2,)), dma((MATE + 2,)),
             ],
             compiler_params=pltpu.CompilerParams(
                 collective_id=0, has_side_effects=True, vmem_limit_bytes=63 * 2**20),

time: 443 us -> 440 us (level)
  no operation moved by 1% of the time
where the time goes in v4:
time: 440 us
  Pallas kernels  437 us (99%)
    pallas_call x1, Pallas kernels, step(): pl.pallas_call(functools.partial(kernel, n), out_shape=(jax.ShapeDtypeStr...  419 us
    pallas_call x1, Pallas kernels, step(): pl.pallas_call(functools.partial(copy_kernel, n), out_shape=jax.ShapeDtyp...  17 us
  transfers between devices with their start and end apart: 2, of which 0 were waited for; matrix products, arithmetic and copies ran while one was open for 0% of the time, Pallas kernels for 4%

profile of v4, /device:TPU:112, one launch (start us, length us, event | category | flops | bytes accessed | tf_op | source)
XLA Modules:
  0.0 440.1 jit_solution(16256659799673548343)
XLA Ops:
  0.0 418.5 %shard_map.46 = (bf16[2048,6144]{1,0:T(8,128)(2,1)}, bf16[8,32,1536]{2,1,0:T(8,128)(2,1)}, bf16[8,32,1536]{2,1,0:T(8,128)(2,1)}) custom-call(bf16[2048,6144]{1,0:T(8,128)(2,1)} %x_ref.1, bf16[6144,4096]{1,0:T(8,128)(2,1)} %wg_ref.1, bf16[6144,4096]{1,0:T(8,128)(2,1)} %wu_ref.1, bf16[4096,6144]{1,0:T(8,128)(2,1)} %wd_ref.1), custom_call_target="tpu_custom_call" | custom-call | flops 309237645312 | bytes 1056964608 | tf_op jit(solution)/shard_map/pallas_call | solution.py:400
  418.5 0.7 collective-permute-start
  419.2 2.7 collective-permute-start.1
  421.8 17.0 %shard_map.47.out_in_ref = bf16[2048,6144]{1,0:T(8,128)(2,1)} custom-call(bf16[2048,6144]{1,0:T(8,128)(2,1)} %get-tuple-element.10.y_ref, bf16[8,32,1536]{2,1,0:T(8,128)(2,1)} %get-tuple-element.8.rel_r_ref, bf16[8,32,1536]{2,1,0:T(8,128)(2,1)} %get-tuple-element.9.rel_l_ref), custom_call_target="tpu_custom_call" | custom-call | flops 10000000000 | bytes 50331648 | tf_op jit(solution)/shard_map/pallas_call | solution.py:422
  438.8 0.0 collective-permute-done.from_l_ref
  438.9 0.0 collective-permute-done.1.from_r_ref
  438.9 1.3 shard_map.48
Async XLA Ops:
  418.5 20.3 %collective-permute-start = (bf16[8,32,1536]{2,1,0:T(8,128)(2,1)}, bf16[8,32,1536]{2,1,0:T(8,128)(2,1)S(1)}, u32[]{:S(2)}, u32[]{:S(2)}) collective-permute-start(bf16[8,32,1536]{2,1,0:T(8,128)(2,1)} %get-tuple-element.8.rel_r_ref), channel_id=1, source_target_pairs={{0,1},{1,2},{2,3},{3,0},{4,5},{5,6},{6,7},{7,4},{8,9},{9,10},{10,1... | collective-permute-start | bytes 2359304 | tf_op jit(solution)/shard_map/ppermute | solution.py:419
  419.2 19.7 %collective-permute-start.1 = (bf16[8,32,1536]{2,1,0:T(8,128)(2,1)}, bf16[8,32,1536]{2,1,0:T(8,128)(2,1)S(1)}, u32[]{:S(2)}, u32[]{:S(2)}) collective-permute-start(bf16[8,32,1536]{2,1,0:T(8,128)(2,1)} %get-tuple-element.9.rel_l_ref), channel_id=1, source_target_pairs={{0,3},{1,0},{2,1},{3,2},{4,7},{5,4},{6,5},{7,6},{8,11},{9,8},{10,9... | collective-permute-start | bytes 2359304 | tf_op jit(solution)/shard_map/ppermute | solution.py:420

commit v5 on v4

--- a/solution.py
+++ b/solution.py
@@ -22,10 +22,10 @@
 CHUNK = 128
 
 SCHEDULE = {
-    "pair": [12, 13, 24, 25, 36, 37, 48, 49, 60, 61, 72, 73, 84, 85, 97, 98, 109, 110, 120, 121, 133, 134, 143, 144, 145, 156, 157, 158, 171, 172, 180, 181],
-    "own": [16, 17, 28, 30, 40, 42, 53, 55, 65, 67, 77, 80, 90, 92, 102, 104, 115, 117, 127, 128, 137, 138, 147, 149, 150, 162, 163, 164, 175, 176, 182, 183],
-    "relay": [20, 24, 32, 36, 45, 48, 57, 60, 69, 72, 82, 84, 94, 97, 106, 109, 119, 123, 131, 133, 140, 143, 151, 152, 156, 166, 168, 171, 179, 180, 184, 185],
-    "free": [20, 24, 32, 36, 45, 48, 57, 60, 69, 72, 82, 84, 94, 97, 106, 109, 119, 123, 131, 133, 140, 143, 151, 152, 156, 166, 168, 171, 179, 180, 184, 185],
+    "pair": [12, 13, 24, 25, 36, 37, 48, 49, 61, 62, 72, 73, 86, 87, 97, 98, 109, 110, 120, 121, 132, 133, 144, 145, 146, 156, 157, 158, 168, 169, 180, 181],
+    "own": [16, 17, 28, 31, 41, 43, 54, 56, 66, 69, 79, 80, 92, 94, 104, 105, 117, 118, 129, 130, 138, 139, 149, 150, 151, 165, 166, 167, 179, 180, 182, 183],
+    "relay": [20, 24, 33, 36, 45, 48, 58, 61, 71, 75, 83, 86, 96, 102, 108, 113, 123, 127, 134, 137, 142, 144, 153, 154, 183, 184, 185, 186, 187, 188, 189, 190],
+    "free": [20, 24, 33, 36, 45, 48, 58, 61, 71, 75, 83, 86, 96, 102, 108, 113, 123, 127, 134, 137, 142, 144, 153, 154, 183, 184, 185, 186, 187, 188, 189, 190],
 }
 EVENTS = tuple(SCHEDULE)
 

time: 440 us -> 440 us (level)
  transfers between devices with their start and end apart: 2 -> 2, of which waited for: 0 -> 1; matrix products, arithmetic and copies ran while one was open for 0% -> 0% of each run, Pallas kernels for 4% -> 4%
where the time goes in v5:
time: 440 us
  Pallas kernels  436 us (99%)
    pallas_call x1, Pallas kernels, step(): pl.pallas_call(functools.partial(kernel, n), out_shape=(jax.ShapeDtypeStr...  418 us
    pallas_call x1, Pallas kernels, step(): pl.pallas_call(functools.partial(copy_kernel, n), out_shape=jax.ShapeDtyp...  17 us
  transfers between devices with their start and end apart: 2, of which 1 were waited for; matrix products, arithmetic and copies ran while one was open for 0% of the time, Pallas kernels for 4%

profile of v5, /device:TPU:112, one launch (start us, length us, event | category | flops | bytes accessed | tf_op | source)
XLA Modules:
  0.0 439.6 jit_solution(10727637122356726574)
XLA Ops:
  0.0 417.8 %shard_map.46 = (bf16[2048,6144]{1,0:T(8,128)(2,1)}, bf16[8,32,1536]{2,1,0:T(8,128)(2,1)}, bf16[8,32,1536]{2,1,0:T(8,128)(2,1)}) custom-call(bf16[2048,6144]{1,0:T(8,128)(2,1)} %x_ref.1, bf16[6144,4096]{1,0:T(8,128)(2,1)} %wg_ref.1, bf16[6144,4096]{1,0:T(8,128)(2,1)} %wu_ref.1, bf16[4096,6144]{1,0:T(8,128)(2,1)} %wd_ref.1), custom_call_target="tpu_custom_call" | custom-call | flops 309237645312 | bytes 1056964608 | tf_op jit(solution)/shard_map/pallas_call | solution.py:400
  417.8 0.7 collective-permute-start
  418.4 2.6 collective-permute-start.1
  421.1 17.0 %shard_map.47.out_in_ref = bf16[2048,6144]{1,0:T(8,128)(2,1)} custom-call(bf16[2048,6144]{1,0:T(8,128)(2,1)} %get-tuple-element.10.y_ref, bf16[8,32,1536]{2,1,0:T(8,128)(2,1)} %get-tuple-element.8.rel_r_ref, bf16[8,32,1536]{2,1,0:T(8,128)(2,1)} %get-tuple-element.9.rel_l_ref), custom_call_target="tpu_custom_call" | custom-call | flops 10000000000 | bytes 50331648 | tf_op jit(solution)/shard_map/pallas_call | solution.py:422
  438.1 0.2 collective-permute-done.from_l_ref
  438.3 0.0 collective-permute-done.1.from_r_ref
  438.3 1.3 shard_map.48
Async XLA Ops:
  417.8 20.5 %collective-permute-start = (bf16[8,32,1536]{2,1,0:T(8,128)(2,1)}, bf16[8,32,1536]{2,1,0:T(8,128)(2,1)S(1)}, u32[]{:S(2)}, u32[]{:S(2)}) collective-permute-start(bf16[8,32,1536]{2,1,0:T(8,128)(2,1)} %get-tuple-element.8.rel_r_ref), channel_id=1, source_target_pairs={{0,1},{1,2},{2,3},{3,0},{4,5},{5,6},{6,7},{7,4},{8,9},{9,10},{10,1... | collective-permute-start | bytes 2359304 | tf_op jit(solution)/shard_map/ppermute | solution.py:419
  418.4 19.9 %collective-permute-start.1 = (bf16[8,32,1536]{2,1,0:T(8,128)(2,1)}, bf16[8,32,1536]{2,1,0:T(8,128)(2,1)S(1)}, u32[]{:S(2)}, u32[]{:S(2)}) collective-permute-start(bf16[8,32,1536]{2,1,0:T(8,128)(2,1)} %get-tuple-element.9.rel_l_ref), channel_id=1, source_target_pairs={{0,3},{1,0},{2,1},{3,2},{4,7},{5,4},{6,5},{7,6},{8,11},{9,8},{10,9... | collective-permute-start | bytes 2359304 | tf_op jit(solution)/shard_map/ppermute | solution.py:420

commit v6 on v5

--- a/solution.py
+++ b/solution.py
@@ -361,6 +361,7 @@
             if offset == 1 and i % 2 == 1:
                 src = rel_l_ref.at[i // 2]
             jobs.append((src, units_v.at[i, k], out_ref.at[r, c], ur_sem.at[i, k], uw_sem.at[i, k]))
+    jobs = jobs[full // CHUNK:] + jobs[:full // CHUNK]
     for src, buf, dst, rs, ws in jobs:
         pltpu.make_async_copy(src, buf, rs).start()
     for src, buf, dst, rs, ws in jobs:

time: 440 us -> 440 us (level)
  no operation moved by 1% of the time
where the time goes in v6:
time: 440 us
  Pallas kernels  436 us (99%)
    pallas_call x1, Pallas kernels, step(): pl.pallas_call(functools.partial(kernel, n), out_shape=(jax.ShapeDtypeStr...  418 us
    pallas_call x1, Pallas kernels, step(): pl.pallas_call(functools.partial(copy_kernel, n), out_shape=jax.ShapeDtyp...  16.5 us
  transfers between devices with their start and end apart: 2, of which 1 were waited for; matrix products, arithmetic and copies ran while one was open for 0% of the time, Pallas kernels for 4%

profile of v6, /device:TPU:112, one launch (start us, length us, event | category | flops | bytes accessed | tf_op | source)
XLA Modules:
  0.0 439.6 jit_solution(11532414556174053019)
XLA Ops:
  0.0 417.8 %shard_map.46 = (bf16[2048,6144]{1,0:T(8,128)(2,1)}, bf16[8,32,1536]{2,1,0:T(8,128)(2,1)}, bf16[8,32,1536]{2,1,0:T(8,128)(2,1)}) custom-call(bf16[2048,6144]{1,0:T(8,128)(2,1)} %x_ref.1, bf16[6144,4096]{1,0:T(8,128)(2,1)} %wg_ref.1, bf16[6144,4096]{1,0:T(8,128)(2,1)} %wu_ref.1, bf16[4096,6144]{1,0:T(8,128)(2,1)} %wd_ref.1), custom_call_target="tpu_custom_call" | custom-call | flops 309237645312 | bytes 1056964608 | tf_op jit(solution)/shard_map/pallas_call | solution.py:401
  417.8 0.7 collective-permute-start
  418.4 2.6 collective-permute-start.1
  421.1 16.5 %shard_map.47.out_in_ref = bf16[2048,6144]{1,0:T(8,128)(2,1)} custom-call(bf16[2048,6144]{1,0:T(8,128)(2,1)} %get-tuple-element.10.y_ref, bf16[8,32,1536]{2,1,0:T(8,128)(2,1)} %get-tuple-element.8.rel_r_ref, bf16[8,32,1536]{2,1,0:T(8,128)(2,1)} %get-tuple-element.9.rel_l_ref), custom_call_target="tpu_custom_call" | custom-call | flops 10000000000 | bytes 50331648 | tf_op jit(solution)/shard_map/pallas_call | solution.py:423
  437.6 0.7 collective-permute-done.from_l_ref
  438.3 0.0 collective-permute-done.1.from_r_ref
  438.3 1.3 shard_map.48
Async XLA Ops:
  417.8 20.5 %collective-permute-start = (bf16[8,32,1536]{2,1,0:T(8,128)(2,1)}, bf16[8,32,1536]{2,1,0:T(8,128)(2,1)S(1)}, u32[]{:S(2)}, u32[]{:S(2)}) collective-permute-start(bf16[8,32,1536]{2,1,0:T(8,128)(2,1)} %get-tuple-element.8.rel_r_ref), channel_id=1, source_target_pairs={{0,1},{1,2},{2,3},{3,0},{4,5},{5,6},{6,7},{7,4},{8,9},{9,10},{10,1... | collective-permute-start | bytes 2359304 | tf_op jit(solution)/shard_map/ppermute | solution.py:420
  418.4 19.9 %collective-permute-start.1 = (bf16[8,32,1536]{2,1,0:T(8,128)(2,1)}, bf16[8,32,1536]{2,1,0:T(8,128)(2,1)S(1)}, u32[]{:S(2)}, u32[]{:S(2)}) collective-permute-start(bf16[8,32,1536]{2,1,0:T(8,128)(2,1)} %get-tuple-element.9.rel_l_ref), channel_id=1, source_target_pairs={{0,3},{1,0},{2,1},{3,2},{4,7},{5,4},{6,5},{7,6},{8,11},{9,8},{10,9... | collective-permute-start | bytes 2359304 | tf_op jit(solution)/shard_map/ppermute | solution.py:421
